TPU v7x, 32 devices: a whole 2x2x4 slice. The times are simulated.
32 devices in a mesh: gx: 16 (over z, y, x), gz: 2 (over core).
Axes of the slice: x: 2, y: 2, z: 4, core: 2. Of those that a mesh axis runs over, the one named last changes fastest.
Arguments:
- velocity: float32 [3, 256, 16, 256], P(None, 'gx', 'gz'), may hold values from -6 to 6
- pressure: float32 [256, 16, 256], P('gx', 'gz'), may hold values from 1 to 3
- stress_old: float32 [6, 256, 16, 256], P(None, 'gx', 'gz'), may hold values from -6 to 6
- plastic: float32 [256, 16, 256], P('gx', 'gz'), may hold values from 0 to 2
- viscosity: float32 [256, 16, 256], P('gx', 'gz'), may hold values from 1 to 30
- weak_seed: int32 [256, 16, 256], P('gx', 'gz'), may hold values 0 or 1
Outputs:
- velocity_out: float32 [3, 256, 16, 256], P(None, 'gx', 'gz')
- pressure_out: float32 [256, 16, 256], P('gx', 'gz')
- stress_out: float32 [6, 256, 16, 256], P(None, 'gx', 'gz')
- plastic_out: float32 [256, 16, 256], P('gx', 'gz')
- yield_peak: float32 [2], replicated
All inputs are finite; a program needn't handle non-finite values. No bound on the sum of `weak_seed` on one device may be relied on, other than what follows from the above.
Results may differ from a plain program's by a relative error of at most 0.000059.
Values sent between devices are 32-bit elements; how exact they have to be, the bound alone decides.
A program may use at most 64 MiB of HBM per device.

v0:
```python
import math

import jax
import jax.numpy as jnp
from jax import lax
from jax.sharding import PartitionSpec as P

ITERS = 2


unnormalized_weights = [math.exp(-(k * k) / 18.0) for k in range(-6, 7)]
weight_total = sum(unnormalized_weights)
gauss_weights = [value / weight_total for value in unnormalized_weights]
shear_time_increment = 20.0


def padded_2(block, sides, width):
    for axis, dim in sides:
        count = lax.axis_size(axis)
        forward = [(i, i + 1) for i in range(count - 1)]
        backward = [(target, source) for source, target in forward]
        low = lax.ppermute(
            lax.slice_in_dim(block, block.shape[dim] - width, None, axis=dim), axis, forward
        )
        high = lax.ppermute(lax.slice_in_dim(block, 0, width, axis=dim), axis, backward)
        block = jnp.concatenate([low, block, high], axis=dim)
    return block


def smooth_slices(padded, axis, count):
    total = gauss_weights[0] * lax.slice_in_dim(padded, 0, count, axis=axis)
    for index in range(1, 13):
        total = total + gauss_weights[index] * lax.slice_in_dim(
            padded, index, index + count, axis=axis
        )
    return total


def y_matrix(length):
    places = jnp.arange(length)
    gap = (places[:, None] - places[None, :]).astype(jnp.float32)
    return jnp.where(jnp.abs(gap) <= 6.0, jnp.exp(-gap * gap / 18.0) / weight_total, 0.0)


def smooth_y(field):
    length = field.shape[-1]
    flat = field.reshape(-1, length)
    return jnp.dot(flat, y_matrix(length), precision=lax.Precision.HIGHEST).reshape(field.shape)


def diff_y(field):
    widths = [(0, 0)] * (field.ndim - 1) + [(1, 1)]
    padded = jnp.pad(field, widths)
    return (padded[..., 2:] - padded[..., :-2]) * 0.5


def return_map(
    velocity_x_spacing, velocity_z_spacing, dyv, stress_old, eta_ve, pres, cohesion_strength
):
    divv = velocity_x_spacing[0] + velocity_z_spacing[1] + dyv[2]
    pres = pres - 0.25 * divv
    strain = jnp.stack(
        [
            velocity_x_spacing[0] - divv / 3.0,
            velocity_z_spacing[1] - divv / 3.0,
            dyv[2] - divv / 3.0,
            0.5 * (velocity_x_spacing[1] + velocity_z_spacing[0]),
            0.5 * (velocity_x_spacing[2] + dyv[0]),
            0.5 * (velocity_z_spacing[2] + dyv[1]),
        ]
    )
    trial = 2.0 * eta_ve * (strain + stress_old / (2.0 * shear_time_increment))
    tau_ii = jnp.sqrt(
        0.5 * (trial[0] ** 2 + trial[1] ** 2 + trial[2] ** 2)
        + trial[3] ** 2
        + trial[4] ** 2
        + trial[5] ** 2
    )
    yield_f = tau_ii - 0.5 * jnp.maximum(pres, 0.0) - 0.8660254 * cohesion_strength
    dlam = jnp.maximum(yield_f, 0.0) / (eta_ve + 0.5)
    shrink = 1.0 - eta_ve * dlam / jnp.maximum(tau_ii, 0.5)
    return (pres, trial * shrink, shrink, yield_f, dlam)


def per_device(velocity, pressure, stress_old, plastic, viscosity, weak_seed):
    rows_x = plastic.shape[0]
    rows_z = plastic.shape[1]
    padded = padded_2(plastic, (("gx", 0), ("gz", 1)), 6)
    along_x_direction = smooth_slices(padded, 0, rows_x)
    along_z = smooth_slices(along_x_direction, 1, rows_z)
    smoothed = smooth_y(along_z)
    eta_ve = 1.0 / (1.0 / viscosity + 1.0 / shear_time_increment)
    seeded = weak_seed.astype(jnp.float32)
    cohesion_strength = (1.0 - 0.6 * seeded) / (1.0 + 2.0 * smoothed)
    pres = pressure
    plastic_sum = plastic
    peaks = []
    tau = stress_old
    for step_index in range(ITERS):
        velocity_padded = padded_2(velocity, (("gx", 1), ("gz", 2)), 1)
        velocity_x_spacing = (velocity_padded[:, 2:, 1:-1] - velocity_padded[:, :-2, 1:-1]) * 0.5
        velocity_z_spacing = (velocity_padded[:, 1:-1, 2:] - velocity_padded[:, 1:-1, :-2]) * 0.5
        dyv = diff_y(velocity)
        pres, tau, shrink, yield_f, dlam = return_map(
            velocity_x_spacing, velocity_z_spacing, dyv, stress_old, eta_ve, pres, cohesion_strength
        )
        plastic_sum = plastic_sum + dlam
        maximum_yield_stress, peak_eta = lax.pmax(
            (jnp.max(yield_f), jnp.max(eta_ve * shrink)), ("gx", "gz")
        )
        peaks.append(maximum_yield_stress)
        step = 0.125 / peak_eta
        sxx = tau[0] - pres
        szz = tau[1] - pres
        syy = tau[2] - pres
        xpad = padded_2(jnp.stack([sxx, tau[4], tau[3]]), (("gx", 1),), 1)
        dxs = (xpad[:, 2:] - xpad[:, :-2]) * 0.5
        zpad = padded_2(jnp.stack([tau[3], tau[5], szz]), (("gz", 2),), 1)
        dzs = (zpad[:, :, 2:] - zpad[:, :, :-2]) * 0.5
        dys = diff_y(jnp.stack([tau[4], tau[5], syy]))
        rx = dxs[0] + dzs[0] + dys[0]
        rz = dxs[2] + dzs[2] + dys[1]
        ry = dxs[1] + dzs[1] + dys[2]
        velocity = velocity + step * jnp.stack([rx, rz, ry])
    return (velocity, pres, tau, plastic_sum, jnp.stack(peaks))


def solution(mesh):
    in_specs = (
        P(None, "gx", "gz", None),
        P("gx", "gz", None),
        P(None, "gx", "gz", None),
        P("gx", "gz", None),
        P("gx", "gz", None),
        P("gx", "gz", None),
    )
    out_specs = (
        P(None, "gx", "gz", None),
        P("gx", "gz", None),
        P(None, "gx", "gz", None),
        P("gx", "gz", None),
        P(),
    )
    return jax.shard_map(
        per_device, mesh=mesh, in_specs=in_specs, out_specs=out_specs, check_vma=False
    )
```

profile of v0, /device:TPU:0, one launch (start us, length us, event | category | flops | bytes accessed | tf_op | source)
XLA Modules:
  0.0 162.5 jit_solution(10354299959430779138)
XLA Ops:
  1.4 1.3 collective-permute-start
  2.7 5.5 %collective-permute-start.1 = (f32[3,1,8,256]{3,2,1,0:T(8,128)S(1)}, f32[3,1,8,256]{3,2,1,0:T(8,128)S(1)}, u32[]{:S(2)}, u32[]{:S(2)}) collective-permute-start(f32[3,1,8,256]{3,2,1,0:T(8,128)S(1)} %get-tuple-element.63), channel_id=1, source_target_pairs={{0,2},{2,4},{4,6},{6,8},{8,10},{10,12},{12,14},{14,16},{16,18},{18... | collective-permute-start | bytes 73736 | tf_op jit(solution)/shard_map/ppermute | solution.py:22
  8.2 0.8 fusion.145
  9.1 1.3 collective-permute-start.5
  10.4 5.5 %collective-permute-start.4 = (f32[6,8,256]{2,1,0:T(8,128)S(1)}, f32[6,8,256]{2,1,0:T(8,128)S(1)}, u32[]{:S(2)}, u32[]{:S(2)}) collective-permute-start(f32[6,8,256]{2,1,0:T(8,128)S(1)} %get-tuple-element.72), channel_id=1, source_target_pairs={{0,2},{2,4},{4,6},{6,8},{8,10},{10,12},{12,14},{14,16},{16,18},{18... | collective-permute-start | bytes 147464 | tf_op jit(solution)/shard_map/ppermute | solution.py:22
  15.8 0.9 broadcast_multiply_fusion.2
  17.2 1.3 collective-permute-start.2
  18.5 3.0 %collective-permute-start.3 = (f32[3,18,1,256]{3,2,1,0:T(1,128)S(1)}, f32[3,18,1,256]{3,2,1,0:T(1,128)S(1)}, u32[]{:S(2)}, u32[]{:S(2)}) collective-permute-start(f32[3,18,1,256]{3,2,1,0:T(1,128)S(1)} %get-tuple-element.47), channel_id=1, source_target_pairs={{0,1},{2,3},{4,5},{6,7},{8,9},{10,11},{12,13},{14,15},{16,17},{18,... | collective-permute-start | bytes 165896 | tf_op jit(solution)/shard_map/ppermute | solution.py:22
  21.7 1.3 collective-permute-start.6
  23.0 1.3 collective-permute-start.7
  24.7 1.0 copy-done.3
  30.0 0.8 copy-done.1
  30.9 1.4 collective-permute-start.8
  32.3 5.4 %collective-permute-start.9 = (f32[3,1,8,256]{3,2,1,0:T(8,128)S(1)}, f32[3,1,8,256]{3,2,1,0:T(8,128)S(1)}, u32[]{:S(2)}, u32[]{:S(2)}) collective-permute-start(f32[3,1,8,256]{3,2,1,0:T(8,128)S(1)} %get-tuple-element.56), channel_id=1, source_target_pairs={{0,2},{2,4},{4,6},{6,8},{8,10},{10,12},{12,14},{14,16},{16,18},{18... | collective-permute-start | bytes 73736 | tf_op jit(solution)/shard_map/ppermute | solution.py:22
  37.9 1.3 collective-permute-start.10
  39.2 3.0 %collective-permute-start.11 = (f32[3,16,1,256]{3,2,1,0:T(1,128)S(1)}, f32[3,16,1,256]{3,2,1,0:T(1,128)S(1)}, u32[]{:S(2)}, u32[]{:S(2)}) collective-permute-start(f32[3,16,1,256]{3,2,1,0:T(1,128)S(1)} %get-tuple-element.58), channel_id=1, source_target_pairs={{0,1},{2,3},{4,5},{6,7},{8,9},{10,11},{12,13},{14,15},{16,17},{18,... | collective-permute-start | bytes 147464 | tf_op jit(solution)/shard_map/ppermute | solution.py:22
  42.6 44.8 %pmax.28 = f32[]{:T(128)} all-reduce(f32[]{:T(128)} %get-tuple-element.20), channel_id=1, replica_groups=mesh['gx'=16,'gz'=2] {'gx','gz'}, use_global_device_ids=true, to_apply=%region_1.2 | all-reduce | flops 1 | bytes 8 | tf_op jit(solution)/shard_map/pmax | solution.py:108
  88.5 1.3 collective-permute-start.12
  89.8 4.8 %collective-permute-start.13 = (f32[3,1,8,256]{3,2,1,0:T(8,128)S(1)}, f32[3,1,8,256]{3,2,1,0:T(8,128)S(1)}, u32[]{:S(2)}, u32[]{:S(2)}) collective-permute-start(f32[3,1,8,256]{3,2,1,0:T(8,128)S(1)} %get-tuple-element.54), channel_id=1, source_target_pairs={{0,2},{2,4},{4,6},{6,8},{8,10},{10,12},{12,14},{14,16},{16,18},{18... | collective-permute-start | bytes 73736 | tf_op jit(solution)/shard_map/ppermute | solution.py:22
  94.6 1.5 collective-permute-done.13
  96.2 1.3 collective-permute-start.14
  97.5 3.0 %collective-permute-start.15 = (f32[3,18,1,256]{3,2,1,0:T(1,128)S(1)}, f32[3,18,1,256]{3,2,1,0:T(1,128)S(1)}, u32[]{:S(2)}, u32[]{:S(2)}) collective-permute-start(f32[3,18,1,256]{3,2,1,0:T(1,128)S(1)} %get-tuple-element.45), channel_id=1, source_target_pairs={{0,1},{2,3},{4,5},{6,7},{8,9},{10,11},{12,13},{14,15},{16,17},{18,... | collective-permute-start | bytes 165896 | tf_op jit(solution)/shard_map/ppermute | solution.py:22
  100.5 0.9 collective-permute-done.15
  102.1 0.8 add_add_fusion
  103.8 0.8 copy-done
  104.7 1.4 collective-permute-start.16
  106.1 5.4 %collective-permute-start.17 = (f32[3,1,8,256]{3,2,1,0:T(8,128)S(1)}, f32[3,1,8,256]{3,2,1,0:T(8,128)S(1)}, u32[]{:S(2)}, u32[]{:S(2)}) collective-permute-start(f32[3,1,8,256]{3,2,1,0:T(8,128)S(1)} %get-tuple-element.49), channel_id=1, source_target_pairs={{0,2},{2,4},{4,6},{6,8},{8,10},{10,12},{12,14},{14,16},{16,18},{18... | collective-permute-start | bytes 73736 | tf_op jit(solution)/shard_map/ppermute | solution.py:22
  111.6 1.3 collective-permute-start.18
  112.9 3.0 %collective-permute-start.19 = (f32[3,16,1,256]{3,2,1,0:T(1,128)S(1)}, f32[3,16,1,256]{3,2,1,0:T(1,128)S(1)}, u32[]{:S(2)}, u32[]{:S(2)}) collective-permute-start(f32[3,16,1,256]{3,2,1,0:T(1,128)S(1)} %get-tuple-element.51), channel_id=1, source_target_pairs={{0,1},{2,3},{4,5},{6,7},{8,9},{10,11},{12,13},{14,15},{16,17},{18,... | collective-permute-start | bytes 147464 | tf_op jit(solution)/shard_map/ppermute | solution.py:22
  116.4 42.4 %all-reduce.4 = (f32[]{:T(128)}, f32[1]{0:T(128)}, f32[1]{0:T(128)}) all-reduce(f32[]{:T(128)} %get-tuple-element.16, f32[1]{0:T(128)} %bitcast.18, f32[1]{0:T(128)} %bitcast.17), channel_id=1, replica_groups=mesh['gx'=16,'gz'=2] {'gx','gz'}, use_global_device_ids=true, to_apply=%region_3.4 | all-reduce | flops 3 | bytes 24 | tf_op jit(solution)/shard_map/pmax | solution.py:108
  158.8 1.8 %pad_maximum_fusion.52 = f32[2]{0:T(128)} fusion(f32[1]{0:T(128)} %get-tuple-element.6, f32[1]{0:T(128)} %get-tuple-element.7), kind=kLoop, calls=%fused_computation.272 | loop fusion | flops 2 | bytes 16 | tf_op jit(solution)/shard_map/stack | solution.py:125
  161.6 0.8 fusion.39
  (89 shorter events, 9.0 us)
Async XLA Ops:
  0.6 16.2 %copy-start.2 = (f32[3,16,8,256]{3,2,1,0:T(8,128)S(1)}, f32[3,16,8,256]{3,2,1,0:T(8,128)}, u32[]{:S(2)}) copy-start(f32[3,16,8,256]{3,2,1,0:T(8,128)} %param.6) | copy-start | bytes 1179652
  1.4 15.4 %collective-permute-start = (f32[3,1,8,256]{3,2,1,0:T(8,128)S(1)}, f32[3,1,8,256]{3,2,1,0:T(8,128)S(1)}, u32[]{:S(2)}, u32[]{:S(2)}) collective-permute-start(f32[3,1,8,256]{3,2,1,0:T(8,128)S(1)} %get-tuple-element.62), channel_id=1, source_target_pairs={{2,0},{4,2},{6,4},{8,6},{10,8},{12,10},{14,12},{16,14},{18,16},{20... | collective-permute-start | bytes 73736 | tf_op jit(solution)/shard_map/ppermute | solution.py:25
  2.7 14.0 %collective-permute-start.1 = (f32[3,1,8,256]{3,2,1,0:T(8,128)S(1)}, f32[3,1,8,256]{3,2,1,0:T(8,128)S(1)}, u32[]{:S(2)}, u32[]{:S(2)}) collective-permute-start(f32[3,1,8,256]{3,2,1,0:T(8,128)S(1)} %get-tuple-element.63), channel_id=1, source_target_pairs={{0,2},{2,4},{4,6},{6,8},{8,10},{10,12},{12,14},{14,16},{16,18},{18... | collective-permute-start | bytes 73736 | tf_op jit(solution)/shard_map/ppermute | solution.py:22
  9.1 12.5 %collective-permute-start.5 = (f32[6,8,256]{2,1,0:T(8,128)S(1)}, f32[6,8,256]{2,1,0:T(8,128)S(1)}, u32[]{:S(2)}, u32[]{:S(2)}) collective-permute-start(f32[6,8,256]{2,1,0:T(8,128)S(1)} %get-tuple-element.71), channel_id=1, source_target_pairs={{2,0},{4,2},{6,4},{8,6},{10,8},{12,10},{14,12},{16,14},{18,16},{20... | collective-permute-start | bytes 147464 | tf_op jit(solution)/shard_map/ppermute | solution.py:25
  10.4 11.2 %collective-permute-start.4 = (f32[6,8,256]{2,1,0:T(8,128)S(1)}, f32[6,8,256]{2,1,0:T(8,128)S(1)}, u32[]{:S(2)}, u32[]{:S(2)}) collective-permute-start(f32[6,8,256]{2,1,0:T(8,128)S(1)} %get-tuple-element.72), channel_id=1, source_target_pairs={{0,2},{2,4},{4,6},{6,8},{8,10},{10,12},{12,14},{14,16},{16,18},{18... | collective-permute-start | bytes 147464 | tf_op jit(solution)/shard_map/ppermute | solution.py:22
  17.1 4.5 %copy-start.5 = (f32[16,8,256]{2,1,0:T(8,128)S(1)}, f32[16,8,256]{2,1,0:T(8,128)}, u32[]{:S(2)}) copy-start(f32[16,8,256]{2,1,0:T(8,128)} %param.9) | copy-start | bytes 393220
  17.2 7.1 %collective-permute-start.2 = (f32[3,18,1,256]{3,2,1,0:T(1,128)S(1)}, f32[3,18,1,256]{3,2,1,0:T(1,128)S(1)}, u32[]{:S(2)}, u32[]{:S(2)}) collective-permute-start(f32[3,18,1,256]{3,2,1,0:T(1,128)S(1)} %get-tuple-element.46), channel_id=1, source_target_pairs={{1,0},{3,2},{5,4},{7,6},{9,8},{11,10},{13,12},{15,14},{17,16},{19,... | collective-permute-start | bytes 165896 | tf_op jit(solution)/shard_map/ppermute | solution.py:25
  18.5 5.8 %collective-permute-start.3 = (f32[3,18,1,256]{3,2,1,0:T(1,128)S(1)}, f32[3,18,1,256]{3,2,1,0:T(1,128)S(1)}, u32[]{:S(2)}, u32[]{:S(2)}) collective-permute-start(f32[3,18,1,256]{3,2,1,0:T(1,128)S(1)} %get-tuple-element.47), channel_id=1, source_target_pairs={{0,1},{2,3},{4,5},{6,7},{8,9},{10,11},{12,13},{14,15},{16,17},{18,... | collective-permute-start | bytes 165896 | tf_op jit(solution)/shard_map/ppermute | solution.py:22
  21.7 4.1 %collective-permute-start.6 = (f32[28,6,256]{2,1,0:T(8,128)S(1)}, f32[28,6,256]{2,1,0:T(8,128)S(1)}, u32[]{:S(2)}, u32[]{:S(2)}) collective-permute-start(f32[28,6,256]{2,1,0:T(8,128)S(1)} %get-tuple-element.64), channel_id=1, source_target_pairs={{0,1},{2,3},{4,5},{6,7},{8,9},{10,11},{12,13},{14,15},{16,17},{18,... | collective-permute-start | bytes 516104 | tf_op jit(solution)/shard_map/ppermute | solution.py:22
  23.0 3.4 %collective-permute-start.7 = (f32[28,6,256]{2,1,0:T(8,128)S(1)}, f32[28,6,256]{2,1,0:T(8,128)S(1)}, u32[]{:S(2)}, u32[]{:S(2)}) collective-permute-start(f32[28,6,256]{2,1,0:T(8,128)S(1)} %get-tuple-element.65), channel_id=1, source_target_pairs={{1,0},{3,2},{5,4},{7,6},{9,8},{11,10},{13,12},{15,14},{17,16},{19,... | collective-permute-start | bytes 516104 | tf_op jit(solution)/shard_map/ppermute | solution.py:25
  24.5 1.1 copy-start.3
  26.5 0.9 copy-start.8
  27.4 0.9 copy-start.7
  28.3 0.9 copy-start.4
  30.0 0.9 copy-start.1
  30.9 11.3 %slice-start.1 = ((f32[6,16,8,256]{3,2,1,0:T(8,128)}), f32[2,16,8,256]{3,2,1,0:T(8,128)S(1)}, s32[]{:S(2)}) async-start(f32[6,16,8,256]{3,2,1,0:T(8,128)} %copy-done.1), calls=%async_computation.1 | async-start | bytes 524288 | tf_op jit(solution)/shard_map/slice | solution.py:116
  30.9 57.2 %collective-permute-start.8 = (f32[3,1,8,256]{3,2,1,0:T(8,128)S(1)}, f32[3,1,8,256]{3,2,1,0:T(8,128)S(1)}, u32[]{:S(2)}, u32[]{:S(2)}) collective-permute-start(f32[3,1,8,256]{3,2,1,0:T(8,128)S(1)} %get-tuple-element.55), channel_id=1, source_target_pairs={{2,0},{4,2},{6,4},{8,6},{10,8},{12,10},{14,12},{16,14},{18,16},{20... | collective-permute-start | bytes 73736 | tf_op jit(solution)/shard_map/ppermute | solution.py:25
  32.3 55.8 %collective-permute-start.9 = (f32[3,1,8,256]{3,2,1,0:T(8,128)S(1)}, f32[3,1,8,256]{3,2,1,0:T(8,128)S(1)}, u32[]{:S(2)}, u32[]{:S(2)}) collective-permute-start(f32[3,1,8,256]{3,2,1,0:T(8,128)S(1)} %get-tuple-element.56), channel_id=1, source_target_pairs={{0,2},{2,4},{4,6},{6,8},{8,10},{10,12},{12,14},{14,16},{16,18},{18... | collective-permute-start | bytes 73736 | tf_op jit(solution)/shard_map/ppermute | solution.py:22
  37.9 50.3 %collective-permute-start.10 = (f32[3,16,1,256]{3,2,1,0:T(1,128)S(1)}, f32[3,16,1,256]{3,2,1,0:T(1,128)S(1)}, u32[]{:S(2)}, u32[]{:S(2)}) collective-permute-start(f32[3,16,1,256]{3,2,1,0:T(1,128)S(1)} %get-tuple-element.57), channel_id=1, source_target_pairs={{1,0},{3,2},{5,4},{7,6},{9,8},{11,10},{13,12},{15,14},{17,16},{19,... | collective-permute-start | bytes 147464 | tf_op jit(solution)/shard_map/ppermute | solution.py:25
  39.2 49.0 %collective-permute-start.11 = (f32[3,16,1,256]{3,2,1,0:T(1,128)S(1)}, f32[3,16,1,256]{3,2,1,0:T(1,128)S(1)}, u32[]{:S(2)}, u32[]{:S(2)}) collective-permute-start(f32[3,16,1,256]{3,2,1,0:T(1,128)S(1)} %get-tuple-element.58), channel_id=1, source_target_pairs={{0,1},{2,3},{4,5},{6,7},{8,9},{10,11},{12,13},{14,15},{16,17},{18,... | collective-permute-start | bytes 147464 | tf_op jit(solution)/shard_map/ppermute | solution.py:22
  88.5 6.1 %collective-permute-start.12 = (f32[3,1,8,256]{3,2,1,0:T(8,128)S(1)}, f32[3,1,8,256]{3,2,1,0:T(8,128)S(1)}, u32[]{:S(2)}, u32[]{:S(2)}) collective-permute-start(f32[3,1,8,256]{3,2,1,0:T(8,128)S(1)} %get-tuple-element.53), channel_id=1, source_target_pairs={{2,0},{4,2},{6,4},{8,6},{10,8},{12,10},{14,12},{16,14},{18,16},{20... | collective-permute-start | bytes 73736 | tf_op jit(solution)/shard_map/ppermute | solution.py:25
  89.8 6.3 %collective-permute-start.13 = (f32[3,1,8,256]{3,2,1,0:T(8,128)S(1)}, f32[3,1,8,256]{3,2,1,0:T(8,128)S(1)}, u32[]{:S(2)}, u32[]{:S(2)}) collective-permute-start(f32[3,1,8,256]{3,2,1,0:T(8,128)S(1)} %get-tuple-element.54), channel_id=1, source_target_pairs={{0,2},{2,4},{4,6},{6,8},{8,10},{10,12},{12,14},{14,16},{16,18},{18... | collective-permute-start | bytes 73736 | tf_op jit(solution)/shard_map/ppermute | solution.py:22
  96.2 4.3 %collective-permute-start.14 = (f32[3,18,1,256]{3,2,1,0:T(1,128)S(1)}, f32[3,18,1,256]{3,2,1,0:T(1,128)S(1)}, u32[]{:S(2)}, u32[]{:S(2)}) collective-permute-start(f32[3,18,1,256]{3,2,1,0:T(1,128)S(1)} %get-tuple-element.44), channel_id=1, source_target_pairs={{1,0},{3,2},{5,4},{7,6},{9,8},{11,10},{13,12},{15,14},{17,16},{19,... | collective-permute-start | bytes 165896 | tf_op jit(solution)/shard_map/ppermute | solution.py:25
  97.5 3.9 %collective-permute-start.15 = (f32[3,18,1,256]{3,2,1,0:T(1,128)S(1)}, f32[3,18,1,256]{3,2,1,0:T(1,128)S(1)}, u32[]{:S(2)}, u32[]{:S(2)}) collective-permute-start(f32[3,18,1,256]{3,2,1,0:T(1,128)S(1)} %get-tuple-element.45), channel_id=1, source_target_pairs={{0,1},{2,3},{4,5},{6,7},{8,9},{10,11},{12,13},{14,15},{16,17},{18,... | collective-permute-start | bytes 165896 | tf_op jit(solution)/shard_map/ppermute | solution.py:22
  102.9 0.8 copy-start.6
  103.7 0.9 copy-start
  104.7 11.3 %slice-start = ((f32[6,16,8,256]{3,2,1,0:T(8,128)}), f32[2,16,8,256]{3,2,1,0:T(8,128)S(1)}, s32[]{:S(2)}) async-start(f32[6,16,8,256]{3,2,1,0:T(8,128)} %copy-done), calls=%async_computation | async-start | bytes 524288 | tf_op jit(solution)/shard_map/slice | solution.py:116
  104.7 56.7 %collective-permute-start.16 = (f32[3,1,8,256]{3,2,1,0:T(8,128)S(1)}, f32[3,1,8,256]{3,2,1,0:T(8,128)S(1)}, u32[]{:S(2)}, u32[]{:S(2)}) collective-permute-start(f32[3,1,8,256]{3,2,1,0:T(8,128)S(1)} %get-tuple-element.48), channel_id=1, source_target_pairs={{2,0},{4,2},{6,4},{8,6},{10,8},{12,10},{14,12},{16,14},{18,16},{20... | collective-permute-start | bytes 73736 | tf_op jit(solution)/shard_map/ppermute | solution.py:25
  106.1 55.2 %collective-permute-start.17 = (f32[3,1,8,256]{3,2,1,0:T(8,128)S(1)}, f32[3,1,8,256]{3,2,1,0:T(8,128)S(1)}, u32[]{:S(2)}, u32[]{:S(2)}) collective-permute-start(f32[3,1,8,256]{3,2,1,0:T(8,128)S(1)} %get-tuple-element.49), channel_id=1, source_target_pairs={{0,2},{2,4},{4,6},{6,8},{8,10},{10,12},{12,14},{14,16},{16,18},{18... | collective-permute-start | bytes 73736 | tf_op jit(solution)/shard_map/ppermute | solution.py:22
  111.6 49.7 %collective-permute-start.18 = (f32[3,16,1,256]{3,2,1,0:T(1,128)S(1)}, f32[3,16,1,256]{3,2,1,0:T(1,128)S(1)}, u32[]{:S(2)}, u32[]{:S(2)}) collective-permute-start(f32[3,16,1,256]{3,2,1,0:T(1,128)S(1)} %get-tuple-element.50), channel_id=1, source_target_pairs={{1,0},{3,2},{5,4},{7,6},{9,8},{11,10},{13,12},{15,14},{17,16},{19,... | collective-permute-start | bytes 147464 | tf_op jit(solution)/shard_map/ppermute | solution.py:25
  112.9 48.4 %collective-permute-start.19 = (f32[3,16,1,256]{3,2,1,0:T(1,128)S(1)}, f32[3,16,1,256]{3,2,1,0:T(1,128)S(1)}, u32[]{:S(2)}, u32[]{:S(2)}) collective-permute-start(f32[3,16,1,256]{3,2,1,0:T(1,128)S(1)} %get-tuple-element.51), channel_id=1, source_target_pairs={{0,1},{2,3},{4,5},{6,7},{8,9},{10,11},{12,13},{14,15},{16,17},{18,... | collective-permute-start | bytes 147464 | tf_op jit(solution)/shard_map/ppermute | solution.py:22
where the time goes:
time: 163 us; the launch traced here: 162 us
  blocking collectives  87.2 us (53%)
  starting transfers between devices  53.2 us (33%)
  other arithmetic  10.1 us (6%)
  local copies, waits for them, and re-layouts  5.63 us (3%)
  waiting for transfers between devices  2.96 us (2%)
  between operations  2.75 us (2%)
    pmax x2, blocking collectives, per_device(): lax.pmax((jnp.max(yield_f), jnp.max(eta_ve * shrink)), ('gx', 'gz'))  87.2 us
    ppermute x10, starting transfers between devices, padded_2(): lax.ppermute(lax.slice_in_dim(block, block.shape[dim] - width, None, axis...  40.1 us
    ppermute x10, starting transfers between devices, padded_2(): lax.ppermute(lax.slice_in_dim(block, 0, width, axis=dim), axis, backward)  13.2 us
    unnamed x21, local copies, waits for them, and re-layouts  3.8 us
  transfers between devices with their start and end apart: 20, of which 3 were waited for; matrix products, arithmetic and copies ran while one was open for 3% of the time, Pallas kernels for 0%

commit v1 on v0

v1 whole, which is shorter than its diff:
```python
import functools
import math

import jax
import jax.numpy as jnp
from jax import lax
from jax.experimental import pallas as pl
from jax.experimental.pallas import tpu as pltpu
from jax.sharding import PartitionSpec as P

ITERS = 2
REACH = 6
MESH = pl.DeviceIdType.MESH

unnormalized_weights = [math.exp(-(k * k) / 18.0) for k in range(-REACH, REACH + 1)]
weight_total = sum(unnormalized_weights)
gauss_weights = [value / weight_total for value in unnormalized_weights]
shear_time_increment = 20.0


def kernel(
    gx_count,
    gz_count,
    vel_in,
    pres_in,
    old_in,
    plas_in,
    visc_in,
    weak_in,
    vel_out,
    pres_out,
    stress_out,
    plas_out,
    peak_out,
    V,
    PR,
    OLD,
    PLX,
    VI,
    WK,
    ETA,
    COH,
    PL,
    YM,
    GX,
    GZH,
    SM,
    VZE,
    VZH,
    SX,
    TZ,
    SZE,
    SZH,
    RP,
    RH,
    R,
    RZE,
    RZH,
    TAU,
    PK,
    in_sem,
    out_sem,
    send_sem,
    recv_sem,
    pk_send,
    pk_recv,
):
    rows, nz, ny = PR.shape
    gx = lax.axis_index("gx")
    gz = lax.axis_index("gz")
    me = gx * gz_count + gz
    total = gx_count * gz_count
    has = {
        "xl": gx > 0,
        "xh": gx < gx_count - 1,
        "zl": gz > 0,
        "zh": gz < gz_count - 1,
    }
    target = {
        "xl": (gx - 1, gz),
        "xh": (gx + 1, gz),
        "zl": (gx, gz - 1),
        "zh": (gx, gz + 1),
    }
    opposite = {"xl": "xh", "xh": "xl", "zl": "zh", "zh": "zl"}

    barrier = pltpu.get_barrier_semaphore()

    def greet(step, carry):
        other = lax.rem(me + step, total)
        pl.semaphore_signal(
            barrier,
            inc=1,
            device_id=(other // gz_count, lax.rem(other, gz_count)),
            device_id_type=MESH,
        )
        return carry

    lax.fori_loop(1, total, greet, 0)

    loads = [
        pltpu.make_async_copy(plas_in, PLX.at[pl.ds(REACH, rows)], in_sem.at[0]),
        pltpu.make_async_copy(vel_in, V.at[:, pl.ds(1, rows)], in_sem.at[1]),
        pltpu.make_async_copy(visc_in, VI, in_sem.at[2]),
        pltpu.make_async_copy(weak_in, WK, in_sem.at[3]),
        pltpu.make_async_copy(old_in, OLD, in_sem.at[4]),
        pltpu.make_async_copy(pres_in, PR, in_sem.at[5]),
    ]
    for copy in loads:
        copy.start()

    count = [0]

    def exchange(side, source, landing):
        slot = count[0]
        count[0] += 1
        copy = pltpu.make_async_remote_copy(
            src_ref=source,
            dst_ref=landing,
            send_sem=send_sem.at[slot],
            recv_sem=recv_sem.at[slot],
            device_id=target[side],
            device_id_type=MESH,
        )

        @pl.when(has[side])
        def _():
            copy.start()

        return side, copy

    def wait_sent(pair):
        side, copy = pair

        @pl.when(has[side])
        def _():
            copy.wait_send()

    def wait_got(pair):
        side, copy = pair

        @pl.when(has[opposite[side]])
        def _():
            copy.wait_recv()

    def zero_unless(side, ref):
        @pl.when(jnp.logical_not(has[side]))
        def _():
            ref[...] = jnp.zeros(ref.shape, ref.dtype)

    zero_unless("xl", PLX.at[pl.ds(0, REACH)])
    zero_unless("xh", PLX.at[pl.ds(rows + REACH, REACH)])
    zero_unless("xl", V.at[:, pl.ds(0, 1)])
    zero_unless("xh", V.at[:, pl.ds(rows + 1, 1)])
    zero_unless("zl", GZH.at[0])
    zero_unless("zh", GZH.at[1])
    for buf in (VZH.at[0], RZH.at[0], SZH.at[0, 0], SZH.at[1, 0]):
        zero_unless("zl", buf)
    for buf in (VZH.at[1], RZH.at[1], SZH.at[0, 1], SZH.at[1, 1]):
        zero_unless("zh", buf)
    for it in range(ITERS):
        zero_unless("xl", SX.at[it, :, pl.ds(0, 1)])
        zero_unless("xh", SX.at[it, :, pl.ds(rows + 1, 1)])

    loads[0].wait()
    pl.semaphore_wait(barrier, total - 1)
    plas_copies = [
        exchange("xh", PLX.at[pl.ds(rows, REACH)], PLX.at[pl.ds(0, REACH)]),
        exchange("xl", PLX.at[pl.ds(REACH, REACH)], PLX.at[pl.ds(rows + REACH, REACH)]),
    ]
    loads[1].wait()
    vel_copies = [
        exchange("xh", V.at[:, pl.ds(rows, 1)], V.at[:, pl.ds(0, 1)]),
        exchange("xl", V.at[:, pl.ds(1, 1)], V.at[:, pl.ds(rows + 1, 1)]),
    ]

    def vel_edges(x, carry):
        for c in range(3):
            row = V[c, x + 1]
            VZE[0, c, x] = row[0:1]
            VZE[1, c, x] = row[nz - 1 : nz]
        return carry

    lax.fori_loop(0, rows, vel_edges, 0)
    vz_copies = [
        exchange("zh", VZE.at[1], VZH.at[0]),
        exchange("zl", VZE.at[0], VZH.at[1]),
    ]

    places_a = lax.broadcasted_iota(jnp.int32, (ny, ny), 0)
    places_b = lax.broadcasted_iota(jnp.int32, (ny, ny), 1)
    gap = (places_a - places_b).astype(jnp.float32)
    YM[...] = jnp.where(
        jnp.abs(gap) <= float(REACH), jnp.exp(-gap * gap / 18.0) / weight_total, 0.0
    )
    for copy in loads[2:]:
        copy.wait()

    def prepare(x, carry):
        eta = VI[x]
        ETA[x] = shear_time_increment * eta / (eta + shear_time_increment)
        return carry

    lax.fori_loop(0, rows, prepare, 0)

    sub = lax.broadcasted_iota(jnp.int32, (nz, ny), 0)
    lane = lax.broadcasted_iota(jnp.int32, (nz, ny), 1)

    for pair in plas_copies:
        wait_got(pair)

    def smooth_x(x, carry):
        total_ = gauss_weights[REACH] * PLX[x + REACH]
        for k in range(1, REACH + 1):
            total_ = total_ + gauss_weights[REACH + k] * (PLX[x + REACH - k] + PLX[x + REACH + k])
        GX[x] = total_
        PL[x] = PLX[x + REACH]
        return carry

    lax.fori_loop(0, rows, smooth_x, 0)
    gz_copies = [
        exchange("zh", GX, GZH.at[0]),
        exchange("zl", GX, GZH.at[1]),
    ]
    for pair in gz_copies:
        wait_got(pair)

    def smooth_z(x, carry):
        own, low, high = GX[x], GZH[0, x], GZH[1, x]
        total_ = gauss_weights[REACH] * own
        for k in range(1, REACH + 1):
            above = pltpu.roll(jnp.where(sub >= k, own, high), nz - k, 0)
            below = pltpu.roll(jnp.where(sub < nz - k, own, low), k, 0)
            total_ = total_ + gauss_weights[REACH + k] * (above + below)
        SM[pl.ds(pl.multiple_of(x * nz, nz), nz)] = total_
        return carry

    lax.fori_loop(0, rows, smooth_z, 0)
    smoothed = jnp.dot(SM[...], YM[...], precision=lax.Precision.HIGHEST, preferred_element_type=jnp.float32)
    SM[...] = smoothed

    def cohesion(x, carry):
        seeded = WK[x].astype(jnp.float32)
        value = SM[pl.ds(pl.multiple_of(x * nz, nz), nz)]
        COH[x] = 0.8660254 * ((1.0 - 0.6 * seeded) / (1.0 + 2.0 * value))
        return carry

    lax.fori_loop(0, rows, cohesion, 0)

    for pair in vel_copies + vz_copies:
        wait_got(pair)

    def dy(f):
        up = jnp.where(lane < ny - 1, pltpu.roll(f, ny - 1, 1), 0.0)
        down = jnp.where(lane > 0, pltpu.roll(f, 1, 1), 0.0)
        return (up - down) * 0.5

    def dz(f, low, high):
        up = pltpu.roll(jnp.where(sub >= 1, f, jnp.broadcast_to(high, f.shape)), nz - 1, 0)
        down = pltpu.roll(jnp.where(sub < nz - 1, f, jnp.broadcast_to(low, f.shape)), 1, 0)
        return (up - down) * 0.5

    stores = []
    for it in range(ITERS):
        last = it == ITERS - 1

        def stress_row(x, carry, it=it, last=last):
            most_f, most_eta = carry
            vx, vz, vy = V[0, x + 1], V[1, x + 1], V[2, x + 1]
            dx_v = [(V[c, x + 2] - V[c, x]) * 0.5 for c in range(3)]
            dz_v = [
                dz(f, VZH[0, c, x], VZH[1, c, x]) for c, f in enumerate((vx, vz, vy))
            ]
            dy_v = [dy(f) for f in (vx, vz, vy)]
            div = dx_v[0] + dz_v[1] + dy_v[2]
            third = div * (1.0 / 3.0)
            pres = PR[x] - 0.25 * div
            PR[x] = pres
            strain = (
                dx_v[0] - third,
                dz_v[1] - third,
                dy_v[2] - third,
                0.5 * (dx_v[1] + dz_v[0]),
                0.5 * (dx_v[2] + dy_v[0]),
                0.5 * (dz_v[2] + dy_v[1]),
            )
            eta = ETA[x]
            twice = 2.0 * eta
            trial = [
                twice * (strain[c] + OLD[c, x] * (0.5 / shear_time_increment)) for c in range(6)
            ]
            tau_ii = jnp.sqrt(
                0.5 * (trial[0] * trial[0] + trial[1] * trial[1] + trial[2] * trial[2])
                + trial[3] * trial[3]
                + trial[4] * trial[4]
                + trial[5] * trial[5]
            )
            yield_f = tau_ii - 0.5 * jnp.maximum(pres, 0.0) - COH[x]
            dlam = jnp.maximum(yield_f, 0.0) / (eta + 0.5)
            shrink = 1.0 - eta * dlam / jnp.maximum(tau_ii, 0.5)
            tau = [shrink * value for value in trial]
            PL[x] = PL[x] + dlam
            if last:
                for c in range(6):
                    TAU[c, x] = tau[c]
            SX[it, 0, x + 1] = tau[0] - pres
            SX[it, 1, x + 1] = tau[3]
            SX[it, 2, x + 1] = tau[4]
            szz = tau[1] - pres
            TZ[0, x] = szz
            TZ[1, x] = tau[5]
            TZ[2, x] = tau[2] - pres
            for c, f in enumerate((tau[3], szz, tau[5])):
                SZE[it, 0, c, x] = f[0:1]
                SZE[it, 1, c, x] = f[nz - 1 : nz]
            return jnp.maximum(most_f, yield_f), jnp.maximum(most_eta, eta * shrink)

        start = jnp.full((nz, ny), -jnp.inf, jnp.float32)
        most_f, most_eta = lax.fori_loop(0, rows, stress_row, (start, start))
        PK[it, me] = jnp.concatenate(
            [jnp.max(most_f, axis=0, keepdims=True), jnp.max(most_eta, axis=0, keepdims=True)],
            axis=0,
        )

        def tell(step, carry, it=it):
            other = lax.rem(me + step, total)
            pltpu.make_async_remote_copy(
                src_ref=PK.at[it, me],
                dst_ref=PK.at[it, me],
                send_sem=pk_send.at[it],
                recv_sem=pk_recv.at[it],
                device_id=(other // gz_count, lax.rem(other, gz_count)),
                device_id_type=MESH,
            ).start()
            return carry

        lax.fori_loop(1, total, tell, 0)
        sx_copies = [
            exchange("xh", SX.at[it, :, pl.ds(rows, 1)], SX.at[it, :, pl.ds(0, 1)]),
            exchange("xl", SX.at[it, :, pl.ds(1, 1)], SX.at[it, :, pl.ds(rows + 1, 1)]),
        ]
        sz_copies = [
            exchange("zh", SZE.at[it, 1], SZH.at[it, 0]),
            exchange("zl", SZE.at[it, 0], SZH.at[it, 1]),
        ]
        if last:
            stores += [
                pltpu.make_async_copy(TAU, stress_out, out_sem.at[0]),
                pltpu.make_async_copy(PR, pres_out, out_sem.at[1]),
                pltpu.make_async_copy(PL, plas_out, out_sem.at[2]),
            ]
            for copy in stores:
                copy.start()

        for pair in sz_copies:
            wait_got(pair)

        def in_row(x, it=it):
            txz, txy = SX[it, 1, x + 1], SX[it, 2, x + 1]
            szz, tzy, syy = TZ[0, x], TZ[1, x], TZ[2, x]
            z_terms = [
                dz(f, SZH[it, 0, c, x], SZH[it, 1, c, x]) for c, f in enumerate((txz, szz, tzy))
            ]
            y_terms = [dy(f) for f in (txy, tzy, syy)]
            return [a + b for a, b in zip(z_terms, y_terms)]

        r_copies = []
        if not last:
            low_row, high_row = in_row(0), in_row(rows - 1)
            for c in range(3):
                RP[0, c] = low_row[c] + 0.5 * SX[it, c, 2]
                RP[1, c] = high_row[c] - 0.5 * SX[it, c, rows - 1]
            r_copies += [
                exchange("xh", RP.at[1], RH.at[0]),
                exchange("xl", RP.at[0], RH.at[1]),
            ]
        for pair in sx_copies:
            wait_got(pair)

        def residual_row(x, carry, it=it, last=last):
            terms = in_row(x)
            for c in range(3):
                value = terms[c] + (SX[it, c, x + 2] - SX[it, c, x]) * 0.5
                R[c, x] = value
                if not last:
                    RZE[0, c, x] = value[0:1]
                    RZE[1, c, x] = value[nz - 1 : nz]
            return carry

        lax.fori_loop(0, rows, residual_row, 0)
        if not last:
            r_copies += [
                exchange("zh", RZE.at[1], RZH.at[0]),
                exchange("zl", RZE.at[0], RZH.at[1]),
            ]
            for pair in vel_copies:
                wait_sent(pair)
            for pair in r_copies:
                wait_got(pair)

        others = PK.at[it, pl.ds(0, total - 1)]
        arrived = pltpu.make_async_copy(others, others, pk_recv.at[it])
        arrived.wait()
        peaks = jnp.max(PK[it], axis=0)
        step = 0.125 / jnp.max(peaks[1:2], axis=1, keepdims=True)

        def velocity_row(x, carry):
            for c in range(3):
                V[c, x + 1] = V[c, x + 1] + step * R[c, x]
            return carry

        lax.fori_loop(0, rows, velocity_row, 0)
        if last:
            copy = pltpu.make_async_copy(V.at[:, pl.ds(1, rows)], vel_out, out_sem.at[3])
            copy.start()
            stores.append(copy)
        else:

            @pl.when(has["xl"])
            def _(it=it, step=step):
                for c in range(3):
                    V[c, 0] = V[c, 0] + step * (RH[0, c] + 0.5 * SX[it, c, 1])

            @pl.when(has["xh"])
            def _(it=it, step=step):
                for c in range(3):
                    V[c, rows + 1] = V[c, rows + 1] + step * (RH[1, c] - 0.5 * SX[it, c, rows])

            def edge_row(x, carry):
                for c in range(3):
                    for side in range(2):
                        VZH[side, c, x] = VZH[side, c, x] + step * RZH[side, c, x]
                return carry

            lax.fori_loop(0, rows, edge_row, 0)
        peak_out[it] = jnp.max(peaks[0:1])
        for pair in sx_copies + sz_copies + r_copies:
            wait_sent(pair)
        pltpu.make_async_copy(others, others, pk_send.at[it]).wait()

    for pair in plas_copies + vz_copies + gz_copies:
        wait_sent(pair)
    for copy in stores:
        copy.wait()


def solution(mesh):
    gx_count, gz_count = mesh.shape["gx"], mesh.shape["gz"]
    total = gx_count * gz_count

    def per_device(velocity, pressure, stress_old, plastic, viscosity, weak_seed):
        rows, nz, ny = pressure.shape
        cells = (rows, nz, ny)
        f32 = jnp.float32
        vm = lambda *shape: pltpu.VMEM(shape, f32)
        copies = 6 + 2 + 4 * ITERS + 4 * (ITERS - 1)
        anywhere = pl.BlockSpec(memory_space=pl.ANY)
        return pl.pallas_call(
            functools.partial(kernel, gx_count, gz_count),
            out_shape=(
                jax.ShapeDtypeStruct(velocity.shape, f32),
                jax.ShapeDtypeStruct(pressure.shape, f32),
                jax.ShapeDtypeStruct(stress_old.shape, f32),
                jax.ShapeDtypeStruct(plastic.shape, f32),
                jax.ShapeDtypeStruct((ITERS,), f32),
            ),
            in_specs=[anywhere] * 6,
            out_specs=(anywhere,) * 4 + (pl.BlockSpec(memory_space=pltpu.SMEM),),
            scratch_shapes=[
                vm(3, rows + 2, nz, ny),
                vm(*cells),
                vm(6, *cells),
                vm(rows + 2 * REACH, nz, ny),
                vm(*cells),
                pltpu.VMEM(cells, jnp.int32),
                vm(*cells),
                vm(*cells),
                vm(*cells),
                vm(ny, ny),
                vm(*cells),
                vm(2, *cells),
                vm(rows * nz, ny),
                vm(2, 3, rows, 1, ny),
                vm(2, 3, rows, 1, ny),
                vm(ITERS, 3, rows + 2, nz, ny),
                vm(3, *cells),
                vm(ITERS, 2, 3, rows, 1, ny),
                vm(ITERS, 2, 3, rows, 1, ny),
                vm(2, 3, nz, ny),
                vm(2, 3, nz, ny),
                vm(3, *cells),
                vm(2, 3, rows, 1, ny),
                vm(2, 3, rows, 1, ny),
                vm(6, *cells),
                vm(ITERS, total, 2, ny),
                pltpu.SemaphoreType.DMA((6,)),
                pltpu.SemaphoreType.DMA((4,)),
                pltpu.SemaphoreType.DMA((copies,)),
                pltpu.SemaphoreType.DMA((copies,)),
                pltpu.SemaphoreType.DMA((ITERS,)),
                pltpu.SemaphoreType.DMA((ITERS,)),
            ],
            compiler_params=pltpu.CompilerParams(collective_id=0, has_side_effects=True),
        )(velocity, pressure, stress_old, plastic, viscosity, weak_seed)

    in_specs = (
        P(None, "gx", "gz", None),
        P("gx", "gz", None),
        P(None, "gx", "gz", None),
        P("gx", "gz", None),
        P("gx", "gz", None),
        P("gx", "gz", None),
    )
    out_specs = (
        P(None, "gx", "gz", None),
        P("gx", "gz", None),
        P(None, "gx", "gz", None),
        P("gx", "gz", None),
        P(),
    )
    return jax.shard_map(
        per_device, mesh=mesh, in_specs=in_specs, out_specs=out_specs, check_vma=False
    )
```

time: 163 us -> 37.3 us (0.23)
  blocking collectives: 87.2 us -> 0 us
  starting transfers between devices: 53.2 us -> 0 us
  Pallas kernels: 0 us -> 30.8 us
  other arithmetic: 10.1 us -> 0 us
  waiting for transfers between devices: 2.96 us -> 0 us
  between operations: 2.75 us -> 0.65 us
    pmax x2 -> x0, blocking collectives: 87.2 us -> none  [per_device(): lax.pmax((jnp.max(yield_f), jnp.max(eta_ve * shrink)), ('gx', 'gz'))]
    ppermute x20 -> x0, starting transfers between devices: 53.2 us -> none  [the longest x10 40.1 us: padded_2(): lax.ppermute(lax.slice_in_dim(block, block.shape[dim] - width, None, axis...]
    pallas_call x0 -> x1, Pallas kernels: none -> 30.8 us  [per_device(): pl.pallas_call(functools.partial(kernel, gx_count, gz_count), out_shape=(...]
    ppermute x20 -> x0, waiting for transfers between devices: 2.96 us -> none  [the longest x10 2.37 us: padded_2(): lax.ppermute(lax.slice_in_dim(block, block.shape[dim] - width, None, axis...]
    mul x11 -> x0, other arithmetic: 2.62 us -> none  [the longest x3 1.2 us: return_map(): trial = 2.0 * eta_ve * (strain + stress_old / (2.0 * shear_time_increment))]
    another operation x7 -> x0, other arithmetic: 2.37 us -> none  [the longest x1 1.83 us: per_device(): return (velocity, pres, tau, plastic_sum, jnp.stack(peaks))]
    add x6 -> x0, other arithmetic: 2.15 us -> none  [the longest x2 0.89 us: per_device(): velocity = velocity + step * jnp.stack([rx, rz, ry])]
    reduce_max x3 -> x0, other arithmetic: 2.12 us -> none  [the longest x2 1.39 us: per_device(): jnp.max(eta_ve * shrink)]
  transfers between devices with their start and end apart: 20 -> 0, of which waited for: 3 -> 0; matrix products, arithmetic and copies ran while one was open for 3% -> 0% of each run, Pallas kernels for 0% -> 0%
where the time goes in v1:
time: 37.3 us; the launch traced here: 37.1 us
  Pallas kernels  30.8 us (83%)
  local copies, waits for them, and re-layouts  5.61 us (15%)
  between operations  0.65 us (2%)
    pallas_call x1, Pallas kernels, per_device(): pl.pallas_call(functools.partial(kernel, gx_count, gz_count), out_shape=(...  30.8 us
    unnamed x11, local copies, waits for them, and re-layouts  5.61 us

profile of v1, /device:TPU:0, one launch (start us, length us, event | category | flops | bytes accessed | tf_op | source)
XLA Modules:
  0.0 37.1 jit_solution(4423571549054856814)
XLA Ops:
  0.6 30.8 %shard_map.101 = (f32[3,16,8,256]{3,2,1,0:T(8,128)}, f32[16,8,256]{2,1,0:T(8,128)}, f32[6,16,8,256]{3,2,1,0:T(8,128)}, f32[16,8,256]{2,1,0:T(8,128)}, f32[2]{0:T(128)}) custom-call(f32[3,16,8,256]{3,2,1,0:T(8,128)} %vel_in.1, f32[16,8,256]{2,1,0:T(8,128)} %pres_in.1, f32[6,16,8,256]{3,2,1,0:T(8,128)} %old_in.1, f32[16,8,256]{2,1,0:T(8,128)} %plas_in.1, ...), custom_call_target="tpu_custom_call" | custom-call | tf_op jit(solution)/shard_map/pallas_call | solution.py:458
  31.5 0.0 copy-start
  31.5 1.8 %copy.16 = f32[3,16,8,256]{3,2,1,0:T(8,128)} copy(f32[3,16,8,256]{3,2,1,0:T(8,128)} %get-tuple-element.10) | data formatting | bytes 786432
  33.3 1.6 %copy.17 = f32[16,8,256]{2,1,0:T(8,128)} copy(f32[16,8,256]{2,1,0:T(8,128)} %get-tuple-element.11) | data formatting | bytes 262144
  34.9 0.0 copy-done
  34.9 0.0 copy-start.1
  34.9 0.9 %copy.18 = f32[6,16,8,256]{3,2,1,0:T(8,128)} copy(f32[6,16,8,256]{3,2,1,0:T(8,128)S(1)} %copy-done) | data formatting | bytes 1572864
  35.8 0.1 copy-done.1
  35.9 0.0 copy-start.2
  35.9 0.7 %copy.19 = f32[16,8,256]{2,1,0:T(8,128)} copy(f32[16,8,256]{2,1,0:T(8,128)S(1)} %copy-done.1) | data formatting | bytes 262144
  36.6 0.0 copy-done.2
  36.6 0.5 %copy.20 = f32[2]{0:T(128)} copy(f32[2]{0:T(128)S(1)} %copy-done.2) | data formatting | bytes 16
Async XLA Ops:
  31.5 3.4 %copy-start = (f32[6,16,8,256]{3,2,1,0:T(8,128)S(1)}, f32[6,16,8,256]{3,2,1,0:T(8,128)}, u32[]{:S(2)}) copy-start(f32[6,16,8,256]{3,2,1,0:T(8,128)} %get-tuple-element.12) | copy-start | bytes 2359300
  34.9 1.0 %copy-start.1 = (f32[16,8,256]{2,1,0:T(8,128)S(1)}, f32[16,8,256]{2,1,0:T(8,128)}, u32[]{:S(2)}) copy-start(f32[16,8,256]{2,1,0:T(8,128)} %get-tuple-element.13) | copy-start | bytes 393220
  35.9 0.7 %copy-start.2 = (f32[2]{0:T(128)S(1)}, f32[2]{0:T(128)}, u32[]{:S(2)}) copy-start(f32[2]{0:T(128)} %get-tuple-element.14) | copy-start | bytes 28

commit v2 on v1

v2 whole, which is shorter than its diff:
```python
import functools
import math

import jax
import jax.numpy as jnp
from jax import lax
from jax.experimental import pallas as pl
from jax.experimental.pallas import tpu as pltpu
from jax.sharding import PartitionSpec as P

ITERS = 2
REACH = 6
BLOCK = 2
MESH = pl.DeviceIdType.MESH

unnormalized_weights = [math.exp(-(k * k) / 18.0) for k in range(-REACH, REACH + 1)]
weight_total = sum(unnormalized_weights)
gauss_weights = [value / weight_total for value in unnormalized_weights]
shear_time_increment = 20.0


def kernel(
    gx_count,
    gz_count,
    vel_in,
    pres_in,
    old_in,
    plas_in,
    visc_in,
    weak_in,
    VOUT,
    PR,
    TAU,
    PL,
    peak_out,
    V,
    PIN,
    OLD,
    PLX,
    VI,
    WK,
    ETA,
    COH,
    YM,
    GX,
    GZH,
    SM,
    VZE,
    VZH,
    SX,
    TZ,
    SZE,
    SZH,
    RP,
    RH,
    R,
    RZE,
    RZH,
    TB,
    PK,
    in_sem,
    send_sem,
    recv_sem,
    pk_send,
    pk_recv,
):
    rows, nz, ny = PR.shape
    gx = lax.axis_index("gx")
    gz = lax.axis_index("gz")
    me = gx * gz_count + gz
    total = gx_count * gz_count
    has = {
        "xl": gx > 0,
        "xh": gx < gx_count - 1,
        "zl": gz > 0,
        "zh": gz < gz_count - 1,
    }
    target = {
        "xl": (gx - 1, gz),
        "xh": (gx + 1, gz),
        "zl": (gx, gz - 1),
        "zh": (gx, gz + 1),
    }
    opposite = {"xl": "xh", "xh": "xl", "zl": "zh", "zh": "zl"}

    barrier = pltpu.get_barrier_semaphore()

    def greet(step, carry):
        other = lax.rem(me + step, total)
        pl.semaphore_signal(
            barrier,
            inc=1,
            device_id=(other // gz_count, lax.rem(other, gz_count)),
            device_id_type=MESH,
        )
        return carry

    lax.fori_loop(1, total, greet, 0)

    loads = [
        pltpu.make_async_copy(plas_in, PLX.at[pl.ds(REACH, rows)], in_sem.at[0]),
        pltpu.make_async_copy(vel_in, V.at[:, pl.ds(1, rows)], in_sem.at[1]),
        pltpu.make_async_copy(visc_in, VI, in_sem.at[2]),
        pltpu.make_async_copy(weak_in, WK, in_sem.at[3]),
        pltpu.make_async_copy(old_in, OLD, in_sem.at[4]),
        pltpu.make_async_copy(pres_in, PIN, in_sem.at[5]),
    ]
    for copy in loads:
        copy.start()

    count = [0]

    def exchange(side, source, landing):
        slot = count[0]
        count[0] += 1
        copy = pltpu.make_async_remote_copy(
            src_ref=source,
            dst_ref=landing,
            send_sem=send_sem.at[slot],
            recv_sem=recv_sem.at[slot],
            device_id=target[side],
            device_id_type=MESH,
        )

        @pl.when(has[side])
        def _():
            copy.start()

        return side, copy

    def wait_sent(pair):
        side, copy = pair

        @pl.when(has[side])
        def _():
            copy.wait_send()

    def wait_got(pair):
        side, copy = pair

        @pl.when(has[opposite[side]])
        def _():
            copy.wait_recv()

    def zero_unless(side, ref):
        @pl.when(jnp.logical_not(has[side]))
        def _():
            ref[...] = jnp.zeros(ref.shape, ref.dtype)

    zero_unless("xl", PLX.at[pl.ds(0, REACH)])
    zero_unless("xh", PLX.at[pl.ds(rows + REACH, REACH)])
    zero_unless("xl", V.at[:, pl.ds(0, 1)])
    zero_unless("xh", V.at[:, pl.ds(rows + 1, 1)])
    zero_unless("zl", GZH.at[0])
    zero_unless("zh", GZH.at[1])
    for buf in (VZH.at[0], RZH.at[0], SZH.at[0, 0], SZH.at[1, 0]):
        zero_unless("zl", buf)
    for buf in (VZH.at[1], RZH.at[1], SZH.at[0, 1], SZH.at[1, 1]):
        zero_unless("zh", buf)
    for it in range(ITERS):
        zero_unless("xl", SX.at[it, :, pl.ds(0, 1)])
        zero_unless("xh", SX.at[it, :, pl.ds(rows + 1, 1)])

    loads[0].wait()
    pl.semaphore_wait(barrier, total - 1)
    plas_copies = [
        exchange("xh", PLX.at[pl.ds(rows, REACH)], PLX.at[pl.ds(0, REACH)]),
        exchange("xl", PLX.at[pl.ds(REACH, REACH)], PLX.at[pl.ds(rows + REACH, REACH)]),
    ]
    loads[1].wait()
    vel_copies = [
        exchange("xh", V.at[:, pl.ds(rows, 1)], V.at[:, pl.ds(0, 1)]),
        exchange("xl", V.at[:, pl.ds(1, 1)], V.at[:, pl.ds(rows + 1, 1)]),
    ]

    def vel_edges(x, carry):
        for c in range(3):
            row = V[c, x + 1]
            VZE[0, c, x] = row[0:1]
            VZE[1, c, x] = row[nz - 1 : nz]
        return carry

    lax.fori_loop(0, rows, vel_edges, 0)
    vz_copies = [
        exchange("zh", VZE.at[1], VZH.at[0]),
        exchange("zl", VZE.at[0], VZH.at[1]),
    ]

    places_a = lax.broadcasted_iota(jnp.int32, (ny, ny), 0)
    places_b = lax.broadcasted_iota(jnp.int32, (ny, ny), 1)
    gap = (places_a - places_b).astype(jnp.float32)
    YM[...] = jnp.where(
        jnp.abs(gap) <= float(REACH), jnp.exp(-gap * gap / 18.0) / weight_total, 0.0
    )
    for copy in loads[2:]:
        copy.wait()

    def prepare(x, carry):
        eta = VI[x]
        ETA[x] = shear_time_increment * eta / (eta + shear_time_increment)
        return carry

    lax.fori_loop(0, rows, prepare, 0)

    block = next(size for size in (BLOCK, 2, 1) if rows % size == 0)
    many = (block, nz, ny)
    sub = lax.broadcasted_iota(jnp.int32, many, 1)
    lane = lax.broadcasted_iota(jnp.int32, many, 2)

    def over_rows(body, carry=0):
        return lax.fori_loop(0, rows // block, lambda i, state: body(i * block, state), carry)

    def at(x):
        return pl.ds(x, block)

    for pair in plas_copies:
        wait_got(pair)

    def smooth_x(x, carry):
        sum_ = gauss_weights[REACH] * PLX[at(x + REACH)]
        for k in range(1, REACH + 1):
            sum_ = sum_ + gauss_weights[REACH + k] * (PLX[at(x + REACH - k)] + PLX[at(x + REACH + k)])
        GX[at(x)] = sum_
        return carry

    over_rows(smooth_x)
    gz_copies = [
        exchange("zh", GX, GZH.at[0]),
        exchange("zl", GX, GZH.at[1]),
    ]
    for pair in vel_copies + vz_copies:
        wait_got(pair)

    def dy(f):
        up = jnp.where(lane < ny - 1, pltpu.roll(f, ny - 1, 2), 0.0)
        down = jnp.where(lane > 0, pltpu.roll(f, 1, 2), 0.0)
        return (up - down) * 0.5

    def dz(f, low, high):
        up = pltpu.roll(jnp.where(sub >= 1, f, jnp.broadcast_to(high, f.shape)), nz - 1, 1)
        down = pltpu.roll(jnp.where(sub < nz - 1, f, jnp.broadcast_to(low, f.shape)), 1, 1)
        return (up - down) * 0.5

    def trial_stress(x, pres):
        v = [V[c, at(x + 1)] for c in range(3)]
        dx_v = [(V[c, at(x + 2)] - V[c, at(x)]) * 0.5 for c in range(3)]
        dz_v = [dz(f, VZH[0, c, at(x)], VZH[1, c, at(x)]) for c, f in enumerate(v)]
        dy_v = [dy(f) for f in v]
        div = dx_v[0] + dz_v[1] + dy_v[2]
        third = div * (1.0 / 3.0)
        pres = pres - 0.25 * div
        PR[at(x)] = pres
        strain = (
            dx_v[0] - third,
            dz_v[1] - third,
            dy_v[2] - third,
            0.5 * (dx_v[1] + dz_v[0]),
            0.5 * (dx_v[2] + dy_v[0]),
            0.5 * (dz_v[2] + dy_v[1]),
        )
        twice = 2.0 * ETA[at(x)]
        trial = [
            twice * (strain[c] + OLD[c, at(x)] * (0.5 / shear_time_increment)) for c in range(6)
        ]
        tau_ii = jnp.sqrt(
            0.5 * (trial[0] * trial[0] + trial[1] * trial[1] + trial[2] * trial[2])
            + trial[3] * trial[3]
            + trial[4] * trial[4]
            + trial[5] * trial[5]
        )
        return pres, trial, tau_ii

    def first_trial(x, carry):
        _, trial, tau_ii = trial_stress(x, PIN[at(x)])
        for c in range(6):
            TAU[c, at(x)] = trial[c]
        TB[at(x)] = tau_ii
        return carry

    over_rows(first_trial)

    for pair in gz_copies:
        wait_got(pair)

    def smooth_z(x, carry):
        own, low, high = GX[at(x)], GZH[0, at(x)], GZH[1, at(x)]
        sum_ = gauss_weights[REACH] * own
        for k in range(1, REACH + 1):
            above = pltpu.roll(jnp.where(sub >= k, own, high), nz - k, 1)
            below = pltpu.roll(jnp.where(sub < nz - k, own, low), k, 1)
            sum_ = sum_ + gauss_weights[REACH + k] * (above + below)
        SM[at(x)] = sum_
        return carry

    over_rows(smooth_z)
    SM[...] = jnp.dot(
        SM[...].reshape(rows * nz, ny),
        YM[...],
        precision=lax.Precision.HIGHEST,
        preferred_element_type=jnp.float32,
    ).reshape(rows, nz, ny)

    half = ny // 2 if ny % 256 == 0 else ny
    for it in range(ITERS):
        last = it == ITERS - 1

        def stress_row(x, carry, it=it, last=last):
            most_f, most_eta = carry
            if it == 0:
                pres, trial, tau_ii = PR[at(x)], [TAU[c, at(x)] for c in range(6)], TB[at(x)]
                seeded = WK[at(x)].astype(jnp.float32)
                strength = 0.8660254 * ((1.0 - 0.6 * seeded) / (1.0 + 2.0 * SM[at(x)]))
                COH[at(x)] = strength
                plas = PLX[at(x + REACH)]
            else:
                pres, trial, tau_ii = trial_stress(x, PR[at(x)])
                strength = COH[at(x)]
                plas = PL[at(x)]
            eta = ETA[at(x)]
            yield_f = tau_ii - 0.5 * jnp.maximum(pres, 0.0) - strength
            dlam = jnp.maximum(yield_f, 0.0) / (eta + 0.5)
            shrink = 1.0 - eta * dlam / jnp.maximum(tau_ii, 0.5)
            tau = [shrink * value for value in trial]
            PL[at(x)] = plas + dlam
            if last:
                for c in range(6):
                    TAU[c, at(x)] = tau[c]
            SX[it, 0, at(x + 1)] = tau[0] - pres
            SX[it, 1, at(x + 1)] = tau[3]
            SX[it, 2, at(x + 1)] = tau[4]
            szz = tau[1] - pres
            TZ[0, at(x)] = szz
            TZ[1, at(x)] = tau[5]
            TZ[2, at(x)] = tau[2] - pres
            for c, f in enumerate((tau[3], szz, tau[5])):
                SZE[it, 0, c, at(x)] = f[:, 0:1]
                SZE[it, 1, c, at(x)] = f[:, nz - 1 : nz]
            return jnp.maximum(most_f, yield_f), jnp.maximum(most_eta, eta * shrink)

        start = jnp.full(many, -jnp.inf, jnp.float32)
        most_f, most_eta = over_rows(stress_row, (start, start))
        sx_copies = [
            exchange("xh", SX.at[it, :, pl.ds(rows, 1)], SX.at[it, :, pl.ds(0, 1)]),
            exchange("xl", SX.at[it, :, pl.ds(1, 1)], SX.at[it, :, pl.ds(rows + 1, 1)]),
        ]
        sz_copies = [
            exchange("zh", SZE.at[it, 1], SZH.at[it, 0]),
            exchange("zl", SZE.at[it, 0], SZH.at[it, 1]),
        ]

        def folded(most):
            most = jnp.max(jnp.max(most, axis=0), axis=0, keepdims=True)
            return jnp.maximum(most[:, :half], most[:, ny - half :])

        PK[it, me] = jnp.concatenate([folded(most_f), folded(most_eta)], axis=0)

        def tell(step, carry, it=it):
            other = lax.rem(me + step, total)
            pltpu.make_async_remote_copy(
                src_ref=PK.at[it, me],
                dst_ref=PK.at[it, me],
                send_sem=pk_send.at[it],
                recv_sem=pk_recv.at[it],
                device_id=(other // gz_count, lax.rem(other, gz_count)),
                device_id_type=MESH,
            ).start()
            return carry

        lax.fori_loop(1, total, tell, 0)
        for pair in sz_copies:
            wait_got(pair)

        def inner_row(x, carry, it=it):
            txz, txy = SX[it, 1, at(x + 1)], SX[it, 2, at(x + 1)]
            szz, tzy, syy = TZ[0, at(x)], TZ[1, at(x)], TZ[2, at(x)]
            z_terms = [
                dz(f, SZH[it, 0, c, at(x)], SZH[it, 1, c, at(x)])
                for c, f in enumerate((txz, szz, tzy))
            ]
            y_terms = [dy(f) for f in (txy, tzy, syy)]
            for c in range(3):
                R[c, at(x)] = z_terms[c] + y_terms[c]
            return carry

        def add_x(low, high, it=it):
            for c in range(3):
                R[c, low:high] = R[c, low:high] + 0.5 * (
                    SX[it, c, low + 2 : high + 2] - SX[it, c, low:high]
                )

        r_copies = []
        if not last:
            inner_row(0, 0)
            inner_row(rows - block, 0)
            for c in range(3):
                RP[0, c] = R[c, 0] + 0.5 * SX[it, c, 2]
                RP[1, c] = R[c, rows - 1] - 0.5 * SX[it, c, rows - 1]
            r_copies += [
                exchange("xh", RP.at[1], RH.at[0]),
                exchange("xl", RP.at[0], RH.at[1]),
            ]
        over_rows(inner_row)
        add_x(1, rows - 1)
        for pair in sx_copies:
            wait_got(pair)
        add_x(0, 1)
        add_x(rows - 1, rows)
        if not last:

            def edges(x, carry):
                for c in range(3):
                    value = R[c, at(x)]
                    RZE[0, c, at(x)] = value[:, 0:1]
                    RZE[1, c, at(x)] = value[:, nz - 1 : nz]
                return carry

            over_rows(edges)
            r_copies += [
                exchange("zh", RZE.at[1], RZH.at[0]),
                exchange("zl", RZE.at[0], RZH.at[1]),
            ]
            for pair in vel_copies:
                wait_sent(pair)
            for pair in r_copies:
                wait_got(pair)

        others = PK.at[it, pl.ds(0, total - 1)]
        arrived = pltpu.make_async_copy(others, others, pk_recv.at[it])
        arrived.wait()
        peaks = jnp.max(PK[it], axis=0)
        step = 0.125 / jnp.max(peaks[1:2], axis=1, keepdims=True)

        def velocity_row(x, carry):
            for c in range(3):
                value = V[c, at(x + 1)] + step * R[c, at(x)]
                if last:
                    VOUT[c, at(x)] = value
                else:
                    V[c, at(x + 1)] = value
            return carry

        over_rows(velocity_row)
        if not last:

            @pl.when(has["xl"])
            def _(it=it, step=step):
                for c in range(3):
                    V[c, 0] = V[c, 0] + step * (RH[0, c] + 0.5 * SX[it, c, 1])

            @pl.when(has["xh"])
            def _(it=it, step=step):
                for c in range(3):
                    V[c, rows + 1] = V[c, rows + 1] + step * (RH[1, c] - 0.5 * SX[it, c, rows])

            VZH[...] = VZH[...] + step * RZH[...]
        peak_out[it] = jnp.max(peaks[0:1])
        for pair in sx_copies + sz_copies + r_copies:
            wait_sent(pair)
        pltpu.make_async_copy(others, others, pk_send.at[it]).wait()

    for pair in plas_copies + vz_copies + gz_copies:
        wait_sent(pair)


def store_kernel(*refs):
    held, out, sem = refs[:5], refs[5:10], refs[10]
    copies = [pltpu.make_async_copy(a, b, sem.at[i]) for i, (a, b) in enumerate(zip(held, out))]
    for copy in copies:
        copy.start()
    for copy in copies:
        copy.wait()


def solution(mesh):
    gx_count, gz_count = mesh.shape["gx"], mesh.shape["gz"]
    total = gx_count * gz_count

    def per_device(velocity, pressure, stress_old, plastic, viscosity, weak_seed):
        rows, nz, ny = pressure.shape
        cells = (rows, nz, ny)
        f32 = jnp.float32
        vm = lambda *shape: pltpu.VMEM(shape, f32)
        copies = 6 + 2 + 4 * ITERS + 4 * (ITERS - 1)
        anywhere = pl.BlockSpec(memory_space=pl.ANY)
        shapes = (velocity.shape, pressure.shape, stress_old.shape, plastic.shape)
        *held, peaks = pl.pallas_call(
            functools.partial(kernel, gx_count, gz_count),
            out_shape=tuple(vm(*shape) for shape in shapes)
            + (jax.ShapeDtypeStruct((ITERS,), f32),),
            in_specs=[anywhere] * 6,
            out_specs=(pl.BlockSpec(memory_space=pltpu.VMEM),) * 4
            + (pl.BlockSpec(memory_space=pltpu.SMEM),),
            scratch_shapes=[
                vm(3, rows + 2, nz, ny),
                vm(*cells),
                vm(6, *cells),
                vm(rows + 2 * REACH, nz, ny),
                vm(*cells),
                pltpu.VMEM(cells, jnp.int32),
                vm(*cells),
                vm(*cells),
                vm(ny, ny),
                vm(*cells),
                vm(2, *cells),
                vm(*cells),
                vm(2, 3, rows, 1, ny),
                vm(2, 3, rows, 1, ny),
                vm(ITERS, 3, rows + 2, nz, ny),
                vm(3, *cells),
                vm(ITERS, 2, 3, rows, 1, ny),
                vm(ITERS, 2, 3, rows, 1, ny),
                vm(2, 3, nz, ny),
                vm(2, 3, nz, ny),
                vm(3, *cells),
                vm(2, 3, rows, 1, ny),
                vm(2, 3, rows, 1, ny),
                vm(*cells),
                vm(ITERS, total, 2, ny // 2 if ny % 256 == 0 else ny),
                pltpu.SemaphoreType.DMA((6,)),
                pltpu.SemaphoreType.DMA((copies,)),
                pltpu.SemaphoreType.DMA((copies,)),
                pltpu.SemaphoreType.DMA((ITERS,)),
                pltpu.SemaphoreType.DMA((ITERS,)),
            ],
            compiler_params=pltpu.CompilerParams(collective_id=0, has_side_effects=True),
        )(velocity, pressure, stress_old, plastic, viscosity, weak_seed)
        held = [pltpu.with_memory_space_constraint(array, pltpu.VMEM) for array in held]
        return pl.pallas_call(
            store_kernel,
            out_shape=tuple(jax.ShapeDtypeStruct(shape, f32) for shape in shapes)
            + (jax.ShapeDtypeStruct((ITERS,), f32),),
            in_specs=[anywhere] * 5,
            out_specs=(anywhere,) * 5,
            scratch_shapes=[pltpu.SemaphoreType.DMA((5,))],
        )(*held, peaks)

    in_specs = (
        P(None, "gx", "gz", None),
        P("gx", "gz", None),
        P(None, "gx", "gz", None),
        P("gx", "gz", None),
        P("gx", "gz", None),
        P("gx", "gz", None),
    )
    out_specs = (
        P(None, "gx", "gz", None),
        P("gx", "gz", None),
        P(None, "gx", "gz", None),
        P("gx", "gz", None),
        P(),
    )
    return jax.shard_map(
        per_device, mesh=mesh, in_specs=in_specs, out_specs=out_specs, check_vma=False
    )
```

time: 37.3 us -> 27.6 us (0.74)
  local copies, waits for them, and re-layouts: 5.61 us -> 0 us
  Pallas kernels: 30.8 us -> 26.8 us
    unnamed x11 -> x0, local copies, waits for them, and re-layouts: 5.61 us -> none
    pallas_call x1 -> x2, Pallas kernels: 30.8 us -> 26.8 us  [the longest x1 25.7 us: per_device(): pl.pallas_call(functools.partial(kernel, gx_count, gz_count), out_shape=t...]
where the time goes in v2:
time: 27.6 us; the launch traced here: 27.5 us
  Pallas kernels  26.8 us (97%)
  between operations  0.64 us (2%)
    pallas_call x1, Pallas kernels, per_device(): pl.pallas_call(functools.partial(kernel, gx_count, gz_count), out_shape=t...  25.7 us
    pallas_call x1, Pallas kernels, per_device(): pl.pallas_call(store_kernel, out_shape=tuple((jax.ShapeDtypeStruct(shape,...  1.17 us

profile of v2, /device:TPU:0, one launch (start us, length us, event | category | flops | bytes accessed | tf_op | source)
XLA Modules:
  0.0 27.5 jit_solution(119262785882427498)
XLA Ops:
  0.6 25.7 %shard_map.101 = (f32[3,16,8,256]{3,2,1,0:T(8,128)S(1)}, f32[16,8,256]{2,1,0:T(8,128)S(1)}, f32[6,16,8,256]{3,2,1,0:T(8,128)S(1)}, f32[16,8,256]{2,1,0:T(8,128)S(1)}, f32[2]{0:T(128)}) custom-call(f32[3,16,8,256]{3,2,1,0:T(8,128)} %vel_in.1, f32[16,8,256]{2,1,0:T(8,128)} %pres_in.1, f32[6,16,8,256]{3,2,1,0:T(8,128)} %old_in.1, f32[16,8,256]{2,1,0:T(8,128)} %plas_in.1, ...), custom_call_target="tpu_custom_call" | custom-call | tf_op jit(solution)/shard_map/pallas_call | solution.py:486
  26.3 1.2 %shard_map.102 = (f32[3,16,8,256]{3,2,1,0:T(8,128)}, f32[16,8,256]{2,1,0:T(8,128)}, f32[6,16,8,256]{3,2,1,0:T(8,128)}, f32[16,8,256]{2,1,0:T(8,128)}, f32[2]{0:T(128)}) custom-call(f32[3,16,8,256]{3,2,1,0:T(8,128)S(1)} %get-tuple-element.10.refs_0_, f32[16,8,256]{2,1,0:T(8,128)S(1)} %get-tuple-element.11.refs_1_, ...), custom_call_target="tpu_custom_call" | custom-call | tf_op jit(solution)/shard_map/pallas_call | solution.py:528

commit v3 on v2

--- a/solution.py
+++ b/solution.py
@@ -11,6 +11,7 @@
 ITERS = 2
 REACH = 6
 BLOCK = 2
+UNROLL = 1
 MESH = pl.DeviceIdType.MESH
 
 unnormalized_weights = [math.exp(-(k * k) / 18.0) for k in range(-REACH, REACH + 1)]
@@ -85,17 +86,17 @@
 
     barrier = pltpu.get_barrier_semaphore()
 
-    def greet(step, carry):
-        other = lax.rem(me + step, total)
-        pl.semaphore_signal(
-            barrier,
-            inc=1,
-            device_id=(other // gz_count, lax.rem(other, gz_count)),
-            device_id_type=MESH,
-        )
-        return carry
-
-    lax.fori_loop(1, total, greet, 0)
+    def to_others(act):
+        for dz_ in range(gz_count):
+            other_z = gz + dz_
+            other_z = jnp.where(other_z >= gz_count, other_z - gz_count, other_z)
+
+            def body(dx_, carry):
+                other_x = gx + dx_
+                act((jnp.where(other_x >= gx_count, other_x - gx_count, other_x), other_z))
+                return carry
+
+            lax.fori_loop(0 if dz_ else 1, gx_count, body, 0, unroll=UNROLL)
 
     loads = [
         pltpu.make_async_copy(plas_in, PLX.at[pl.ds(REACH, rows)], in_sem.at[0]),
@@ -105,7 +106,14 @@
         pltpu.make_async_copy(old_in, OLD, in_sem.at[4]),
         pltpu.make_async_copy(pres_in, PIN, in_sem.at[5]),
     ]
-    for copy in loads:
+    for copy in loads[:2]:
+        copy.start()
+    to_others(
+        lambda place: pl.semaphore_signal(
+            barrier, inc=1, device_id=place, device_id_type=MESH
+        )
+    )
+    for copy in loads[2:]:
         copy.start()
 
     count = [0]
@@ -162,16 +170,7 @@
         zero_unless("xh", SX.at[it, :, pl.ds(rows + 1, 1)])
 
     loads[0].wait()
-    pl.semaphore_wait(barrier, total - 1)
-    plas_copies = [
-        exchange("xh", PLX.at[pl.ds(rows, REACH)], PLX.at[pl.ds(0, REACH)]),
-        exchange("xl", PLX.at[pl.ds(REACH, REACH)], PLX.at[pl.ds(rows + REACH, REACH)]),
-    ]
     loads[1].wait()
-    vel_copies = [
-        exchange("xh", V.at[:, pl.ds(rows, 1)], V.at[:, pl.ds(0, 1)]),
-        exchange("xl", V.at[:, pl.ds(1, 1)], V.at[:, pl.ds(rows + 1, 1)]),
-    ]
 
     def vel_edges(x, carry):
         for c in range(3):
@@ -181,6 +180,16 @@
         return carry
 
     lax.fori_loop(0, rows, vel_edges, 0)
+    pl.semaphore_wait(barrier, total - 1)
+    plas_copies = [
+        exchange("xh", PLX.at[pl.ds(rows, REACH)], PLX.at[pl.ds(0, REACH)]),
+        exchange("xl", PLX.at[pl.ds(REACH, REACH)], PLX.at[pl.ds(rows + REACH, REACH)]),
+    ]
+    vel_copies = [
+        exchange("xh", V.at[:, pl.ds(rows, 1)], V.at[:, pl.ds(0, 1)]),
+        exchange("xl", V.at[:, pl.ds(1, 1)], V.at[:, pl.ds(rows + 1, 1)]),
+    ]
+
     vz_copies = [
         exchange("zh", VZE.at[1], VZH.at[0]),
         exchange("zl", VZE.at[0], VZH.at[1]),
@@ -301,6 +310,7 @@
     ).reshape(rows, nz, ny)
 
     half = ny // 2 if ny % 256 == 0 else ny
+    tops = []
     for it in range(ITERS):
         last = it == ITERS - 1
 
@@ -354,19 +364,17 @@
 
         PK[it, me] = jnp.concatenate([folded(most_f), folded(most_eta)], axis=0)
 
-        def tell(step, carry, it=it):
-            other = lax.rem(me + step, total)
+        def tell(place, it=it):
             pltpu.make_async_remote_copy(
                 src_ref=PK.at[it, me],
                 dst_ref=PK.at[it, me],
                 send_sem=pk_send.at[it],
                 recv_sem=pk_recv.at[it],
-                device_id=(other // gz_count, lax.rem(other, gz_count)),
+                device_id=place,
                 device_id_type=MESH,
             ).start()
-            return carry
-
-        lax.fori_loop(1, total, tell, 0)
+
+        to_others(tell)
         for pair in sz_copies:
             wait_got(pair)
 
@@ -453,11 +461,12 @@
                     V[c, rows + 1] = V[c, rows + 1] + step * (RH[1, c] - 0.5 * SX[it, c, rows])
 
             VZH[...] = VZH[...] + step * RZH[...]
-        peak_out[it] = jnp.max(peaks[0:1])
+        tops.append(jnp.max(peaks[0:1], axis=1, keepdims=True))
         for pair in sx_copies + sz_copies + r_copies:
             wait_sent(pair)
         pltpu.make_async_copy(others, others, pk_send.at[it]).wait()
 
+    peak_out[...] = jnp.concatenate(tops, axis=1)[0]
     for pair in plas_copies + vz_copies + gz_copies:
         wait_sent(pair)
 
@@ -483,13 +492,11 @@
         copies = 6 + 2 + 4 * ITERS + 4 * (ITERS - 1)
         anywhere = pl.BlockSpec(memory_space=pl.ANY)
         shapes = (velocity.shape, pressure.shape, stress_old.shape, plastic.shape)
-        *held, peaks = pl.pallas_call(
+        held = pl.pallas_call(
             functools.partial(kernel, gx_count, gz_count),
-            out_shape=tuple(vm(*shape) for shape in shapes)
-            + (jax.ShapeDtypeStruct((ITERS,), f32),),
+            out_shape=tuple(vm(*shape) for shape in shapes + ((ITERS,),)),
             in_specs=[anywhere] * 6,
-            out_specs=(pl.BlockSpec(memory_space=pltpu.VMEM),) * 4
-            + (pl.BlockSpec(memory_space=pltpu.SMEM),),
+            out_specs=(pl.BlockSpec(memory_space=pltpu.VMEM),) * 5,
             scratch_shapes=[
                 vm(3, rows + 2, nz, ny),
                 vm(*cells),
@@ -532,7 +539,7 @@
             in_specs=[anywhere] * 5,
             out_specs=(anywhere,) * 5,
             scratch_shapes=[pltpu.SemaphoreType.DMA((5,))],
-        )(*held, peaks)
+        )(*held)
 
     in_specs = (
         P(None, "gx", "gz", None),

time: 27.6 us -> 26.7 us (0.967)
  Pallas kernels: 26.8 us -> 25.9 us
    pallas_call x1, Pallas kernels: 25.7 us -> 24.7 us  [per_device(): pl.pallas_call(functools.partial(kernel, gx_count, gz_count), out_shape=t...]
where the time goes in v3:
time: 26.7 us; the launch traced here: 26.5 us
  Pallas kernels  25.9 us (97%)
  between operations  0.64 us (2%)
    pallas_call x1, Pallas kernels, per_device(): pl.pallas_call(functools.partial(kernel, gx_count, gz_count), out_shape=t...  24.7 us
    pallas_call x1, Pallas kernels, per_device(): pl.pallas_call(store_kernel, out_shape=tuple((jax.ShapeDtypeStruct(shape,...  1.14 us

profile of v3, /device:TPU:0, one launch (start us, length us, event | category | flops | bytes accessed | tf_op | source)
XLA Modules:
  0.0 26.5 jit_solution(13160992501424491210)
XLA Ops:
  0.6 24.7 %shard_map.101 = (f32[3,16,8,256]{3,2,1,0:T(8,128)S(1)}, f32[16,8,256]{2,1,0:T(8,128)S(1)}, f32[6,16,8,256]{3,2,1,0:T(8,128)S(1)}, f32[16,8,256]{2,1,0:T(8,128)S(1)}, f32[2]{0:T(128)S(1)}) custom-call(f32[3,16,8,256]{3,2,1,0:T(8,128)} %vel_in.1, f32[16,8,256]{2,1,0:T(8,128)} %pres_in.1, f32[6,16,8,256]{3,2,1,0:T(8,128)} %old_in.1, f32[16,8,256]{2,1,0:T(8,128)} %plas_in.1, ...), custom_call_target="tpu_custom_call" | custom-call | tf_op jit(solution)/shard_map/pallas_call | solution.py:495
  25.4 1.1 %shard_map.102 = (f32[3,16,8,256]{3,2,1,0:T(8,128)}, f32[16,8,256]{2,1,0:T(8,128)}, f32[6,16,8,256]{3,2,1,0:T(8,128)}, f32[16,8,256]{2,1,0:T(8,128)}, f32[2]{0:T(128)}) custom-call(f32[3,16,8,256]{3,2,1,0:T(8,128)S(1)} %get-tuple-element.10.refs_0_, f32[16,8,256]{2,1,0:T(8,128)S(1)} %get-tuple-element.11.refs_1_, ...), custom_call_target="tpu_custom_call" | custom-call | tf_op jit(solution)/shard_map/pallas_call | solution.py:535
